TPU v7x, 128 devices: a whole 4x4x4 slice. The times are simulated.
128 devices in a mesh: ep: 8 (over y, core), fs: 16 (over z, x).
Axes of the slice: x: 4, y: 4, z: 4, core: 2. Of those that a mesh axis runs over, the one named last changes fastest.
Arguments:
- grads: bfloat16 [8, 8, 256, 14336], P('ep', None, 'fs'), may hold values from -64 to 64
- counts: int32 [8, 8], replicated, may hold values from 16 to 2047
- weight: bfloat16 [8, 256, 14336], P('ep', 'fs'), may hold values from -3 to 3
- mom: float32 [8, 256, 14336], P('ep', 'fs'), may hold values from -64 to 64
- second: float32 [8, 256, 14336], P('ep', 'fs'), may hold values from 0.1 to 10
- in_weight: float32 [6, 32], replicated, may hold values from -2.5 to 2.5
- in_bias: float32 [32], replicated, may hold values from -3 to 3
- out_weight: float32 [32, 2], replicated, may hold values from -1 to 1
- out_bias: float32 [2], replicated, may hold values from -3 to 3
Outputs:
- new_weight: bfloat16 [8, 256, 14336], P('ep')
- new_mom: float32 [8, 256, 14336], P('ep', 'fs')
- new_second: float32 [8, 256, 14336], P('ep', 'fs')
All inputs are finite; a program needn't handle non-finite values.
Results may differ from a plain program's by a relative error of at most 0.0019.
Values may be sent and summed in bfloat16 or wider, within the bound.
A program may use at most 64 MiB of HBM per device.

v0:
```python
import jax
import jax.numpy as jnp
from jax import lax
from jax.sharding import PartitionSpec as P

MOMENTUM_DECAY = 0.9
SECOND_DECAY = 0.99
NORM_EPS = 1e-06
ROOT_EPS = 1e-08
STEP_SCALE = 0.2
EXP_SCALE = 0.5


def from_everyone(value, axis):
    copies = jnp.broadcast_to(value, (lax.axis_size(axis), *value.shape))
    return lax.all_to_all(copies, axis, split_axis=0, concat_axis=0, tiled=True)


def of_everyone(value, axis):
    return from_everyone(value, axis).sum(axis=0)


def in_one(arrays, axis):
    line, at, done = (jnp.concatenate([a.reshape(-1) for a in arrays]), 0, [])
    so_far = of_everyone(line, axis)
    for a in arrays:
        done.append(so_far[at : at + a.size].reshape(a.shape))
        at += a.size
    return tuple(done)


def learned_step(
    gradient,
    mom_next,
    second_next,
    weight,
    grad_norm,
    mom_norm,
    in_weight,
    in_bias,
    out_weight,
    out_bias,
):
    inv_root = lax.rsqrt(second_next + ROOT_EPS)
    features = jnp.stack(
        [
            gradient / grad_norm,
            mom_next / mom_norm,
            mom_next * inv_root,
            gradient * inv_root,
            weight.astype(jnp.float32),
            jnp.broadcast_to(jnp.log(mom_norm), gradient.shape),
        ]
    )
    hidden = jax.nn.relu(
        jnp.einsum("fh,fab->hab", in_weight, features, precision=lax.Precision.HIGHEST)
        + in_bias[:, None, None]
    )
    outputs = (
        jnp.einsum("hk,hab->kab", out_weight, hidden, precision=lax.Precision.HIGHEST)
        + out_bias[:, None, None]
    )
    update = STEP_SCALE * outputs[0] * jnp.exp(EXP_SCALE * outputs[1])
    return (weight.astype(jnp.float32) - update).astype(jnp.bfloat16)


def add_sources(arrived):
    return jnp.sum(arrived.astype(jnp.float32), axis=0)


def per_device(grads, counts, weight, mom, second, in_weight, in_bias, out_weight, out_bias):
    source = lax.axis_index("ep")
    counts_f = counts.astype(jnp.float32)
    totals = jnp.sum(counts_f, axis=0)
    share_row = lax.dynamic_index_in_dim(counts_f, source, 0, keepdims=False) / totals
    weighted = share_row[None, :, None, None] * grads.astype(jnp.float32)
    outgoing = weighted.astype(jnp.bfloat16)
    gradient = add_sources(lax.all_to_all(outgoing, "ep", split_axis=1, concat_axis=0, tiled=True))[
        0
    ]
    mom_here = mom[0]
    second_here = second[0]
    mom_next = MOMENTUM_DECAY * mom_here + (1.0 - MOMENTUM_DECAY) * gradient
    second_next = SECOND_DECAY * second_here + (1.0 - SECOND_DECAY) * gradient * gradient
    entries = gradient.shape[0] * gradient.shape[1] * lax.axis_size("fs")
    grad_sq, mom_sq = in_one((jnp.sum(gradient * gradient), jnp.sum(mom_next * mom_next)), "fs")
    grad_norm = jnp.sqrt(grad_sq / entries + NORM_EPS)
    mom_norm = jnp.sqrt(mom_sq / entries + NORM_EPS)
    width = gradient.shape[1]

    def block_step(items):
        grad_block, mom_block, second_block, weight_block = items
        return learned_step(
            grad_block,
            mom_block,
            second_block,
            weight_block,
            grad_norm,
            mom_norm,
            in_weight,
            in_bias,
            out_weight,
            out_bias,
        )

    blocks = lax.map(
        block_step,
        (
            gradient.reshape(-1, 2, width),
            mom_next.reshape(-1, 2, width),
            second_next.reshape(-1, 2, width),
            weight[0].reshape(-1, 2, width),
        ),
    )
    updated = blocks.reshape(gradient.shape)
    gathered = lax.all_gather(updated[None], "fs", axis=1, tiled=True)
    return (gathered, mom_next[None], second_next[None])


def solution(mesh):
    in_specs = (
        P("ep", None, "fs", None),
        P(),
        P("ep", "fs", None),
        P("ep", "fs", None),
        P("ep", "fs", None),
        P(),
        P(),
        P(),
        P(),
    )
    out_specs = (P("ep", None, None), P("ep", "fs", None), P("ep", "fs", None))
    return jax.shard_map(
        per_device, mesh=mesh, in_specs=in_specs, out_specs=out_specs, check_vma=False
    )
```

profile of v0, /device:TPU:1, one launch (start us, length us, event | category | flops | bytes accessed | tf_op | source)
XLA Modules:
  0.0 246.2 jit_solution(12678078749305325285)
XLA Ops:
  7.2 0.7 convert_reduce_fusion.1
  7.9 0.7 convert_element_type.34
  8.6 4.7 %multiply_convert_fusion = bf16[1,8,16,14336]{3,2,0,1:T(8,128)(2,1)} fusion(bf16[1,8,16,14336]{3,2,1,0:T(8,128)(2,1)} %param.11, f32[8]{0:T(128)S(1)} %bitcast_divide_fusion), kind=kLoop, calls=%fused_computation.22 | loop fusion | flops 5505024 | bytes 7340064 | tf_op jit(solution)/shard_map/convert_element_type | solution.py:77
  13.3 6.1 %all-to-all-start = ((bf16[1,8,16,14336]{3,2,0,1:T(8,128)(2,1)}), bf16[1,8,16,14336]{3,2,0,1:T(8,128)(2,1)}, u32[]{:S(2)}, u32[]{:S(2)}) async-start(bf16[1,8,16,14336]{3,2,0,1:T(8,128)(2,1)} %multiply_convert_fusion), calls=%async_computation | async-start | bytes 7340032 | tf_op jit(solution)/shard_map/all_to_all | solution.py:78
  19.7 42.8 %all-to-all-done = bf16[1,8,16,14336]{3,2,0,1:T(8,128)(2,1)} async-done(((bf16[1,8,16,14336]{3,2,0,1:T(8,128)(2,1)}), bf16[1,8,16,14336]{3,2,0,1:T(8,128)(2,1)}, u32[]{:S(2)}, u32[]{:S(2)}) %all-to-all-start) | async-done | bytes 3670048 | tf_op jit(solution)/shard_map/all_to_all | solution.py:78
  62.5 2.6 %convert_reduce_fusion = f32[16,14336]{1,0:T(8,128)S(1)} fusion(bf16[1,8,16,14336]{3,2,0,1:T(8,128)(2,1)} %all-to-all-done), kind=kLoop, calls=%fused_computation.21 | loop fusion | flops 3440640 | bytes 4587520 | tf_op jit(solution)/shard_map/reduce_sum | solution.py:68
  65.1 1.5 reshape_squeeze.7
  66.6 0.9 multiply_reduce_fusion
  67.5 1.4 pad_maximum_fusion
  68.8 0.6 broadcast_in_dim.18
  69.5 7.6 %all-to-all-start.1 = ((f32[16,1,2]{2,1,0:T(1,128)}), f32[16,1,2]{2,1,0:T(1,128)S(1)}, u32[]{:S(2)}, u32[]{:S(2)}) async-start(f32[16,1,2]{2,1,0:T(1,128)} %broadcast_in_dim.18), calls=%async_computation.1 | async-start | bytes 16384 | tf_op jit(solution)/shard_map/all_to_all | solution.py:16
  77.3 2.9 %fusion.10 = (f32[1,16,14336]{2,1,0:T(8,128)}, f32[1,16,14336]{2,1,0:T(8,128)}, f32[1,16,14336]{2,1,0:T(8,128)}, f32[1,16,14336]{2,1,0:T(8,128)S(1)}) fusion(f32[16,14336]{1,0:T(8,128)S(1)} %convert_reduce_fusion, f32[1,16,14336]{2,1,0:T(8,128)} %param.15, f32[1,16,14336]{2,1,0:T(8,128)S(1)} %copy-done), kind=kLoop, calls=%fused_computation.26 | loop fusion | flops 1605632 | bytes 6422528 | tf_op jit(solution)/shard_map/add | solution.py:84
  80.2 1.7 mul.131
  81.9 0.5 mul.126
  82.5 4.1 %fusion.9 = (f32[8,2,14336]{2,0,1:T(8,128)S(1)}, f32[8,2,14336]{2,0,1:T(8,128)}, f32[8,2,14336]{2,0,1:T(8,128)}) fusion(f32[8,2,14336]{2,1,0:T(2,128)S(1)} %mul.131, f32[8,2,14336]{2,1,0:T(2,128)} %reshape_squeeze.7, f32[8,2,14336]{2,1,0:T(2,128)S(1)} %mul.126), kind=kLoop, calls=%fused_computation.25 | loop fusion | flops 1146880 | bytes 5505024 | tf_op jit(solution)/shard_map/add | solution.py:84
  86.6 0.6 fusion.14
  88.4 75.6 %while.11 = (s32[]{:T(128)}, bf16[8,2,14336]{2,1,0:T(2,128)(2,1)}, bf16[8,2,14336]{2,1,0:T(2,128)(2,1)S(1)}, f32[8,2,14336]{2,0,1:T(8,128)}, f32[]{:T(128)}, /*i...) while((s32[]{:T(128)}, bf16[8,2,14336]{2,1,0:T(2,128)(2,1)}, ...), condition=%wide.region_6.7_spmd, body=%wide.region_5.6_spmd.sunk | while | flops 90316800 | bytes 11298093 | solution.py:106
  88.7 1.8 dynamic-slice_multiply_fusion.3
  90.5 1.1 stack.4
  91.6 3.2 %fusion.28 = f32[32,2,14336]{2,0,1:T(8,128)S(1)} fusion(f32[6,2,14336]{2,0,1:T(8,128)S(1)} %stack.4, f32[32]{0:T(128)S(1)} %get-tuple-element.350, f32[6,32]{1,0:T(8,128)S(1)} %get-tuple-element.349), kind=kOutput, calls=%fused_computation.2.clone.1 | convolution fusion | flops 67895296 | bytes 4359040 | tf_op jit(solution)/shard_map/while/body/eval_jaxpr/fh,fab->hab/dot_general | solution.py:56
  94.8 2.1 fusion.29
  96.9 0.3 fusion.30
  97.2 0.7 copy_dynamic-update-slice_fusion.2
  98.1 1.8 dynamic-slice_multiply_fusion.3
  99.9 1.1 stack.4
  101.1 3.2 %fusion.28 = f32[32,2,14336]{2,0,1:T(8,128)S(1)} fusion(f32[6,2,14336]{2,0,1:T(8,128)S(1)} %stack.4, f32[32]{0:T(128)S(1)} %get-tuple-element.350, f32[6,32]{1,0:T(8,128)S(1)} %get-tuple-element.349), kind=kOutput, calls=%fused_computation.2.clone.1 | convolution fusion | flops 67895296 | bytes 4359040 | tf_op jit(solution)/shard_map/while/body/eval_jaxpr/fh,fab->hab/dot_general | solution.py:56
  104.3 2.1 fusion.29
  106.3 0.3 fusion.30
  106.7 0.7 copy_dynamic-update-slice_fusion.2
  107.6 1.8 dynamic-slice_multiply_fusion.3
  109.4 1.1 stack.4
  110.5 3.2 %fusion.28 = f32[32,2,14336]{2,0,1:T(8,128)S(1)} fusion(f32[6,2,14336]{2,0,1:T(8,128)S(1)} %stack.4, f32[32]{0:T(128)S(1)} %get-tuple-element.350, f32[6,32]{1,0:T(8,128)S(1)} %get-tuple-element.349), kind=kOutput, calls=%fused_computation.2.clone.1 | convolution fusion | flops 67895296 | bytes 4359040 | tf_op jit(solution)/shard_map/while/body/eval_jaxpr/fh,fab->hab/dot_general | solution.py:56
  113.7 2.1 fusion.29
  115.8 0.3 fusion.30
  116.1 0.7 copy_dynamic-update-slice_fusion.2
  117.0 1.8 dynamic-slice_multiply_fusion.3
  118.8 1.1 stack.4
  120.0 3.2 %fusion.28 = f32[32,2,14336]{2,0,1:T(8,128)S(1)} fusion(f32[6,2,14336]{2,0,1:T(8,128)S(1)} %stack.4, f32[32]{0:T(128)S(1)} %get-tuple-element.350, f32[6,32]{1,0:T(8,128)S(1)} %get-tuple-element.349), kind=kOutput, calls=%fused_computation.2.clone.1 | convolution fusion | flops 67895296 | bytes 4359040 | tf_op jit(solution)/shard_map/while/body/eval_jaxpr/fh,fab->hab/dot_general | solution.py:56
  123.2 2.1 fusion.29
  125.2 0.3 fusion.30
  125.5 0.7 copy_dynamic-update-slice_fusion.2
  126.4 1.8 dynamic-slice_multiply_fusion.3
  128.3 1.1 stack.4
  129.4 3.2 %fusion.28 = f32[32,2,14336]{2,0,1:T(8,128)S(1)} fusion(f32[6,2,14336]{2,0,1:T(8,128)S(1)} %stack.4, f32[32]{0:T(128)S(1)} %get-tuple-element.350, f32[6,32]{1,0:T(8,128)S(1)} %get-tuple-element.349), kind=kOutput, calls=%fused_computation.2.clone.1 | convolution fusion | flops 67895296 | bytes 4359040 | tf_op jit(solution)/shard_map/while/body/eval_jaxpr/fh,fab->hab/dot_general | solution.py:56
  132.6 2.1 fusion.29
  135.0 0.7 copy_dynamic-update-slice_fusion.2
  135.9 1.8 dynamic-slice_multiply_fusion.3
  137.7 1.1 stack.4
  138.9 3.2 %fusion.28 = f32[32,2,14336]{2,0,1:T(8,128)S(1)} fusion(f32[6,2,14336]{2,0,1:T(8,128)S(1)} %stack.4, f32[32]{0:T(128)S(1)} %get-tuple-element.350, f32[6,32]{1,0:T(8,128)S(1)} %get-tuple-element.349), kind=kOutput, calls=%fused_computation.2.clone.1 | convolution fusion | flops 67895296 | bytes 4359040 | tf_op jit(solution)/shard_map/while/body/eval_jaxpr/fh,fab->hab/dot_general | solution.py:56
  142.1 2.1 fusion.29
  144.4 0.7 copy_dynamic-update-slice_fusion.2
  145.3 1.8 dynamic-slice_multiply_fusion.3
  147.2 1.1 stack.4
  148.3 3.2 %fusion.28 = f32[32,2,14336]{2,0,1:T(8,128)S(1)} fusion(f32[6,2,14336]{2,0,1:T(8,128)S(1)} %stack.4, f32[32]{0:T(128)S(1)} %get-tuple-element.350, f32[6,32]{1,0:T(8,128)S(1)} %get-tuple-element.349), kind=kOutput, calls=%fused_computation.2.clone.1 | convolution fusion | flops 67895296 | bytes 4359040 | tf_op jit(solution)/shard_map/while/body/eval_jaxpr/fh,fab->hab/dot_general | solution.py:56
  151.5 2.1 fusion.29
  153.9 0.7 copy_dynamic-update-slice_fusion.2
  154.8 1.8 dynamic-slice_multiply_fusion.3
  156.6 1.1 stack.4
  157.8 3.2 %fusion.28 = f32[32,2,14336]{2,0,1:T(8,128)S(1)} fusion(f32[6,2,14336]{2,0,1:T(8,128)S(1)} %stack.4, f32[32]{0:T(128)S(1)} %get-tuple-element.350, f32[6,32]{1,0:T(8,128)S(1)} %get-tuple-element.349), kind=kOutput, calls=%fused_computation.2.clone.1 | convolution fusion | flops 67895296 | bytes 4359040 | tf_op jit(solution)/shard_map/while/body/eval_jaxpr/fh,fab->hab/dot_general | solution.py:56
  161.0 2.1 fusion.29
  163.3 0.7 copy_dynamic-update-slice_fusion.2
  164.0 2.0 broadcast_in_dim_reshape.3
  166.0 66.5 %all-gather.2.cloned.1.call-done = bf16[1,256,14336]{2,1,0:T(8,128)(2,1)} async-done(((bf16[1,16,14336]{2,1,0:T(8,128)(2,1)}), bf16[1,256,14336]{2,1,0:T(8,128)(2,1)}) %all-gather.2.cloned.1.call-update) | async-done | bytes 7340048 | tf_op jit(solution)/shard_map/all_gather | solution.py:116
  232.5 6.9 %copy.86 = bf16[1,256,14336]{2,1,0:T(8,128)(2,1)} copy(bf16[1,256,14336]{2,1,0:T(8,128)(2,1)} %all-gather.2.cloned.1.call-done) | data formatting | bytes 14680064
  (47 shorter events, 3.4 us)
Async XLA Ops:
  13.2 6.1 %copy-start.1 = (bf16[1,16,14336]{2,1,0:T(8,128)(2,1)S(1)}, bf16[1,16,14336]{2,1,0:T(8,128)(2,1)}, u32[]{:S(2)}) copy-start(bf16[1,16,14336]{2,1,0:T(8,128)(2,1)} %param.13) | copy-start | bytes 1376260
  13.3 49.3 %all-to-all-start = ((bf16[1,8,16,14336]{3,2,0,1:T(8,128)(2,1)}), bf16[1,8,16,14336]{3,2,0,1:T(8,128)(2,1)}, u32[]{:S(2)}, u32[]{:S(2)}) async-start(bf16[1,8,16,14336]{3,2,0,1:T(8,128)(2,1)} %multiply_convert_fusion), calls=%async_computation | async-start | bytes 7340032 | tf_op jit(solution)/shard_map/all_to_all | solution.py:78
  19.3 47.3 %copy-start = (f32[1,16,14336]{2,1,0:T(8,128)S(1)}, f32[1,16,14336]{2,1,0:T(8,128)}, u32[]{:S(2)}) copy-start(f32[1,16,14336]{2,1,0:T(8,128)} %param.14) | copy-start | bytes 2752516
  69.5 17.1 %all-to-all-start.1 = ((f32[16,1,2]{2,1,0:T(1,128)}), f32[16,1,2]{2,1,0:T(1,128)S(1)}, u32[]{:S(2)}, u32[]{:S(2)}) async-start(f32[16,1,2]{2,1,0:T(1,128)} %broadcast_in_dim.18), calls=%async_computation.1 | async-start | bytes 16384 | tf_op jit(solution)/shard_map/all_to_all | solution.py:16
  77.1 155.4 %all-gather.2.cloned.1.call-start = ((), (), s32[]{:S(2)}) async-start(), calls=%async_computation.2 | async-start | bytes 7798784 | tf_op jit(solution)/shard_map/all_gather | solution.py:116
  81.9 6.5 %copy-start.2 = (f32[6,32]{1,0:T(8,128)S(1)}, f32[6,32]{1,0:T(8,128)}, u32[]{:S(2)}) copy-start(f32[6,32]{1,0:T(8,128)} %param.16) | copy-start | bytes 2308
  81.9 6.5 %copy-start.3 = (f32[32,2]{0,1:T(2,128)S(1)}, f32[32,2]{0,1:T(2,128)}, u32[]{:S(2)}) copy-start(f32[32,2]{0,1:T(2,128)} %param.18) | copy-start | bytes 772
  81.9 6.5 %copy-start.4 = (f32[32]{0:T(128)S(1)}, f32[32]{0:T(128)}, u32[]{:S(2)}) copy-start(f32[32]{0:T(128)} %param.17) | copy-start | bytes 388
  81.9 6.5 %copy-start.5 = (f32[2]{0:T(128)S(1)}, f32[2]{0:T(128)}, u32[]{:S(2)}) copy-start(f32[2]{0:T(128)} %param.19) | copy-start | bytes 28
Sparse Core Ops, SparseCore 0:
  166.1 66.3 all-gather.1
where the time goes:
time: 247 us; the launch traced here: 246 us
  waiting for transfers between devices  109 us (44%)
  matrix products  42 us (17%)
  other arithmetic  35.8 us (14%)
  local copies, waits for them, and re-layouts  29.4 us (12%)
  between operations  15.4 us (6%)
  starting transfers between devices  13.9 us (6%)
    all_gather x1, waiting for transfers between devices, per_device(): gathered = lax.all_gather(updated[None], 'fs', axis=1, tiled=True)  66.5 us
    all_to_all x1, waiting for transfers between devices, per_device(): lax.all_to_all(outgoing, 'ep', split_axis=1, concat_axis=0, tiled=True)  42.8 us
    dot_general x8, matrix products, learned_step(): jnp.einsum('fh,fab->hab', in_weight, features, precision=lax.Precision.HI...  25.6 us
    dot_general x8, matrix products, learned_step(): jnp.einsum('hk,hab->kab', out_weight, hidden, precision=lax.Precision.HIG...  16.4 us
    mul x8, other arithmetic, learned_step(): gradient * inv_root  14.7 us
    another operation x8, local copies, waits for them, and re-layouts, learned_step(): jnp.stack([gradient / grad_norm, mom_next / mom_norm, mom_next * inv_root...  8.98 us
    all_to_all x1, starting transfers between devices, from_everyone(): return lax.all_to_all(copies, axis, split_axis=0, concat_axis=0, tiled=True)  7.6 us
    unnamed x13, local copies, waits for them, and re-layouts  6.93 us
  transfers between devices with their start and end apart: 3, of which 2 were waited for; matrix products, arithmetic and copies ran while one was open for 4% of the time, Pallas kernels for 0%

commit v1 on v0

--- a/solution.py
+++ b/solution.py
@@ -75,9 +75,10 @@
     share_row = lax.dynamic_index_in_dim(counts_f, source, 0, keepdims=False) / totals
     weighted = share_row[None, :, None, None] * grads.astype(jnp.float32)
     outgoing = weighted.astype(jnp.bfloat16)
-    gradient = add_sources(lax.all_to_all(outgoing, "ep", split_axis=1, concat_axis=0, tiled=True))[
-        0
-    ]
+    _touch_arrays = lambda out_dim, s0, at_axis: jnp.concatenate(
+        lax.all_to_all(jnp.stack(jnp.split(s0, lax.axis_size("ep"), out_dim)), "ep", 0, 0), at_axis
+    )
+    gradient = add_sources(_touch_arrays(1, outgoing, 0))[0]
     mom_here = mom[0]
     second_here = second[0]
     mom_next = MOMENTUM_DECAY * mom_here + (1.0 - MOMENTUM_DECAY) * gradient

time: 247 us -> 252 us (1.020)
  local copies, waits for them, and re-layouts: 29.4 us -> 35.8 us
    unnamed x13 -> x20, local copies, waits for them, and re-layouts: 6.93 us -> 12.5 us
where the time goes in v1:
time: 252 us; the launch traced here: 251 us
  waiting for transfers between devices  109 us (43%)
  matrix products  42 us (17%)
  local copies, waits for them, and re-layouts  35.8 us (14%)
  other arithmetic  33.9 us (13%)
  between operations  15.4 us (6%)
  starting transfers between devices  13.9 us (6%)
    all_gather x1, waiting for transfers between devices, per_device(): gathered = lax.all_gather(updated[None], 'fs', axis=1, tiled=True)  66.5 us
    all_to_all x1, waiting for transfers between devices, per_device(): lax.all_to_all(jnp.stack(jnp.split(s0, lax.axis_size('ep'), out_dim)), 'e...  42.8 us
    dot_general x8, matrix products, learned_step(): jnp.einsum('fh,fab->hab', in_weight, features, precision=lax.Precision.HI...  25.6 us
    dot_general x8, matrix products, learned_step(): jnp.einsum('hk,hab->kab', out_weight, hidden, precision=lax.Precision.HIG...  16.4 us
    mul x8, other arithmetic, learned_step(): gradient * inv_root  14.7 us
    unnamed x20, local copies, waits for them, and re-layouts  12.5 us
    another operation x8, local copies, waits for them, and re-layouts, learned_step(): jnp.stack([gradient / grad_norm, mom_next / mom_norm, mom_next * inv_root...  8.98 us
    all_to_all x1, starting transfers between devices, from_everyone(): return lax.all_to_all(copies, axis, split_axis=0, concat_axis=0, tiled=True)  7.6 us
  transfers between devices with their start and end apart: 3, of which 2 were waited for; matrix products, arithmetic and copies ran while one was open for 4% of the time, Pallas kernels for 0%

profile of v1, /device:TPU:1, one launch (start us, length us, event | category | flops | bytes accessed | tf_op | source)
XLA Modules:
  0.0 250.8 jit_solution(5318484901330291755)
XLA Ops:
  7.2 0.7 convert_reduce_fusion.1
  7.9 0.7 convert_element_type.34
  8.6 2.8 %multiply_convert_fusion = bf16[1,8,16,14336]{3,2,1,0:T(8,128)(2,1)S(1)} fusion(bf16[1,8,16,14336]{3,2,1,0:T(8,128)(2,1)} %param.11, f32[8]{0:T(128)S(1)} %bitcast_divide_fusion), kind=kLoop, calls=%fused_computation.22 | loop fusion | flops 5505024 | bytes 7340064 | tf_op jit(solution)/shard_map/convert_element_type | solution.py:77
  11.4 0.8 fusion.21
  12.2 0.8 fusion.20
  13.0 0.8 fusion.19
  13.8 0.8 fusion.18
  14.6 0.8 fusion.17
  15.4 0.8 fusion.16
  16.2 0.8 fusion.15
  17.0 0.8 fusion.14
  17.8 6.1 %all-to-all-start = ((bf16[8,1,1,16,14336]{4,3,2,1,0:T(8,128)(2,1)}), bf16[8,1,1,16,14336]{4,3,2,1,0:T(8,128)(2,1)}, u32[]{:S(2)}, u32[]{:S(2)}) async-start(bf16[8,1,1,16,14336]{4,3,2,1,0:T(8,128)(2,1)} %fusion.14), calls=%async_computation | async-start | bytes 7340032 | tf_op jit(solution)/shard_map/all_to_all | solution.py:79
  24.2 42.8 %all-to-all-done = bf16[8,1,1,16,14336]{4,3,2,1,0:T(8,128)(2,1)} async-done(((bf16[8,1,1,16,14336]{4,3,2,1,0:T(8,128)(2,1)}), bf16[8,1,1,16,14336]{4,3,2,1,0:T(8,128)(2,1)}, u32[]{:S(2)}, u32[]{:S(2)}) %all-to-all-start) | async-done | bytes 3670048 | tf_op jit(solution)/shard_map/all_to_all | solution.py:79
  67.0 2.6 %convert_reduce_fusion = f32[16,14336]{1,0:T(8,128)S(1)} fusion(bf16[8,1,1,16,14336]{4,3,2,1,0:T(8,128)(2,1)} %all-to-all-done), kind=kLoop, calls=%fused_computation.21 | loop fusion | flops 3440640 | bytes 4587520 | tf_op jit(solution)/shard_map/reduce_sum | solution.py:68
  69.7 1.5 reshape_squeeze.7
  71.2 0.9 multiply_reduce_fusion
  72.0 1.4 pad_maximum_fusion
  74.0 7.6 %all-to-all-start.1 = ((f32[16,1,2]{2,1,0:T(1,128)}), f32[16,1,2]{2,1,0:T(1,128)S(1)}, u32[]{:S(2)}, u32[]{:S(2)}) async-start(f32[16,1,2]{2,1,0:T(1,128)} %broadcast_in_dim.18), calls=%async_computation.1 | async-start | bytes 16384 | tf_op jit(solution)/shard_map/all_to_all | solution.py:16
  81.8 2.9 %fusion.10 = (f32[1,16,14336]{2,1,0:T(8,128)}, f32[1,16,14336]{2,1,0:T(8,128)}, f32[1,16,14336]{2,1,0:T(8,128)}, f32[1,16,14336]{2,1,0:T(8,128)S(1)}) fusion(f32[16,14336]{1,0:T(8,128)S(1)} %convert_reduce_fusion, f32[1,16,14336]{2,1,0:T(8,128)} %param.15, f32[1,16,14336]{2,1,0:T(8,128)S(1)} %copy-done), kind=kLoop, calls=%fused_computation.26 | loop fusion | flops 1605632 | bytes 6422528 | tf_op jit(solution)/shard_map/add | solution.py:85
  84.7 1.7 mul.131
  87.0 4.1 %fusion.9 = (f32[8,2,14336]{2,0,1:T(8,128)S(1)}, f32[8,2,14336]{2,0,1:T(8,128)}, f32[8,2,14336]{2,0,1:T(8,128)}) fusion(f32[8,2,14336]{2,1,0:T(2,128)S(1)} %mul.131, f32[8,2,14336]{2,1,0:T(2,128)} %reshape_squeeze.7, f32[8,2,14336]{2,1,0:T(2,128)S(1)} %mul.126), kind=kLoop, calls=%fused_computation.25 | loop fusion | flops 1146880 | bytes 5505024 | tf_op jit(solution)/shard_map/add | solution.py:85
  93.0 75.6 %while.11 = (s32[]{:T(128)}, bf16[8,2,14336]{2,1,0:T(2,128)(2,1)}, bf16[8,2,14336]{2,1,0:T(2,128)(2,1)S(1)}, f32[8,2,14336]{2,0,1:T(8,128)}, f32[]{:T(128)}, /*i...) while((s32[]{:T(128)}, bf16[8,2,14336]{2,1,0:T(2,128)(2,1)}, ...), condition=%wide.region_6.7_spmd, body=%wide.region_5.6_spmd.sunk | while | flops 90316800 | bytes 11298093 | solution.py:107
  93.2 1.8 dynamic-slice_multiply_fusion.3
  95.0 1.1 stack.46
  96.2 3.2 %fusion.36 = f32[32,2,14336]{2,0,1:T(8,128)S(1)} fusion(f32[6,2,14336]{2,0,1:T(8,128)S(1)} %stack.46, f32[32]{0:T(128)S(1)} %get-tuple-element.337, f32[6,32]{1,0:T(8,128)S(1)} %get-tuple-element.336), kind=kOutput, calls=%fused_computation.2.clone.1 | convolution fusion | flops 67895296 | bytes 4359040 | tf_op jit(solution)/shard_map/while/body/eval_jaxpr/fh,fab->hab/dot_general | solution.py:56
  99.4 2.1 fusion.37
  101.7 0.7 copy_dynamic-update-slice_fusion.2
  102.6 1.8 dynamic-slice_multiply_fusion.3
  104.5 1.1 stack.46
  105.6 3.2 %fusion.36 = f32[32,2,14336]{2,0,1:T(8,128)S(1)} fusion(f32[6,2,14336]{2,0,1:T(8,128)S(1)} %stack.46, f32[32]{0:T(128)S(1)} %get-tuple-element.337, f32[6,32]{1,0:T(8,128)S(1)} %get-tuple-element.336), kind=kOutput, calls=%fused_computation.2.clone.1 | convolution fusion | flops 67895296 | bytes 4359040 | tf_op jit(solution)/shard_map/while/body/eval_jaxpr/fh,fab->hab/dot_general | solution.py:56
  108.8 2.1 fusion.37
  111.2 0.7 copy_dynamic-update-slice_fusion.2
  112.1 1.8 dynamic-slice_multiply_fusion.3
  113.9 1.1 stack.46
  115.1 3.2 %fusion.36 = f32[32,2,14336]{2,0,1:T(8,128)S(1)} fusion(f32[6,2,14336]{2,0,1:T(8,128)S(1)} %stack.46, f32[32]{0:T(128)S(1)} %get-tuple-element.337, f32[6,32]{1,0:T(8,128)S(1)} %get-tuple-element.336), kind=kOutput, calls=%fused_computation.2.clone.1 | convolution fusion | flops 67895296 | bytes 4359040 | tf_op jit(solution)/shard_map/while/body/eval_jaxpr/fh,fab->hab/dot_general | solution.py:56
  118.3 2.1 fusion.37
  120.6 0.7 copy_dynamic-update-slice_fusion.2
  121.5 1.8 dynamic-slice_multiply_fusion.3
  123.4 1.1 stack.46
  124.5 3.2 %fusion.36 = f32[32,2,14336]{2,0,1:T(8,128)S(1)} fusion(f32[6,2,14336]{2,0,1:T(8,128)S(1)} %stack.46, f32[32]{0:T(128)S(1)} %get-tuple-element.337, f32[6,32]{1,0:T(8,128)S(1)} %get-tuple-element.336), kind=kOutput, calls=%fused_computation.2.clone.1 | convolution fusion | flops 67895296 | bytes 4359040 | tf_op jit(solution)/shard_map/while/body/eval_jaxpr/fh,fab->hab/dot_general | solution.py:56
  127.7 2.1 fusion.37
  130.1 0.7 copy_dynamic-update-slice_fusion.2
  131.0 1.8 dynamic-slice_multiply_fusion.3
  132.8 1.1 stack.46
  134.0 3.2 %fusion.36 = f32[32,2,14336]{2,0,1:T(8,128)S(1)} fusion(f32[6,2,14336]{2,0,1:T(8,128)S(1)} %stack.46, f32[32]{0:T(128)S(1)} %get-tuple-element.337, f32[6,32]{1,0:T(8,128)S(1)} %get-tuple-element.336), kind=kOutput, calls=%fused_computation.2.clone.1 | convolution fusion | flops 67895296 | bytes 4359040 | tf_op jit(solution)/shard_map/while/body/eval_jaxpr/fh,fab->hab/dot_general | solution.py:56
  137.2 2.1 fusion.37
  139.5 0.7 copy_dynamic-update-slice_fusion.2
  140.4 1.8 dynamic-slice_multiply_fusion.3
  142.3 1.1 stack.46
  143.4 3.2 %fusion.36 = f32[32,2,14336]{2,0,1:T(8,128)S(1)} fusion(f32[6,2,14336]{2,0,1:T(8,128)S(1)} %stack.46, f32[32]{0:T(128)S(1)} %get-tuple-element.337, f32[6,32]{1,0:T(8,128)S(1)} %get-tuple-element.336), kind=kOutput, calls=%fused_computation.2.clone.1 | convolution fusion | flops 67895296 | bytes 4359040 | tf_op jit(solution)/shard_map/while/body/eval_jaxpr/fh,fab->hab/dot_general | solution.py:56
  146.6 2.1 fusion.37
  149.0 0.7 copy_dynamic-update-slice_fusion.2
  149.9 1.8 dynamic-slice_multiply_fusion.3
  151.7 1.1 stack.46
  152.8 3.2 %fusion.36 = f32[32,2,14336]{2,0,1:T(8,128)S(1)} fusion(f32[6,2,14336]{2,0,1:T(8,128)S(1)} %stack.46, f32[32]{0:T(128)S(1)} %get-tuple-element.337, f32[6,32]{1,0:T(8,128)S(1)} %get-tuple-element.336), kind=kOutput, calls=%fused_computation.2.clone.1 | convolution fusion | flops 67895296 | bytes 4359040 | tf_op jit(solution)/shard_map/while/body/eval_jaxpr/fh,fab->hab/dot_general | solution.py:56
  156.1 2.1 fusion.37
  158.4 0.7 copy_dynamic-update-slice_fusion.2
  159.3 1.8 dynamic-slice_multiply_fusion.3
  161.2 1.1 stack.46
  162.3 3.2 %fusion.36 = f32[32,2,14336]{2,0,1:T(8,128)S(1)} fusion(f32[6,2,14336]{2,0,1:T(8,128)S(1)} %stack.46, f32[32]{0:T(128)S(1)} %get-tuple-element.337, f32[6,32]{1,0:T(8,128)S(1)} %get-tuple-element.336), kind=kOutput, calls=%fused_computation.2.clone.1 | convolution fusion | flops 67895296 | bytes 4359040 | tf_op jit(solution)/shard_map/while/body/eval_jaxpr/fh,fab->hab/dot_general | solution.py:56
  165.5 2.1 fusion.37
  168.6 2.0 broadcast_in_dim_reshape.3
  170.5 66.5 %all-gather.2.cloned.1.call-done = bf16[1,256,14336]{2,1,0:T(8,128)(2,1)} async-done(((bf16[1,16,14336]{2,1,0:T(8,128)(2,1)}), bf16[1,256,14336]{2,1,0:T(8,128)(2,1)}) %all-gather.2.cloned.1.call-update) | async-done | bytes 7340048 | tf_op jit(solution)/shard_map/all_gather | solution.py:117
  237.0 6.9 %copy.82 = bf16[1,256,14336]{2,1,0:T(8,128)(2,1)} copy(bf16[1,256,14336]{2,1,0:T(8,128)(2,1)} %all-gather.2.cloned.1.call-done) | data formatting | bytes 14680064
  (55 shorter events, 7.0 us)
Async XLA Ops:
  17.8 6.1 %copy-start.1 = (bf16[1,16,14336]{2,1,0:T(8,128)(2,1)S(1)}, bf16[1,16,14336]{2,1,0:T(8,128)(2,1)}, u32[]{:S(2)}) copy-start(bf16[1,16,14336]{2,1,0:T(8,128)(2,1)} %param.13) | copy-start | bytes 1376260
  17.8 49.3 %all-to-all-start = ((bf16[8,1,1,16,14336]{4,3,2,1,0:T(8,128)(2,1)}), bf16[8,1,1,16,14336]{4,3,2,1,0:T(8,128)(2,1)}, u32[]{:S(2)}, u32[]{:S(2)}) async-start(bf16[8,1,1,16,14336]{4,3,2,1,0:T(8,128)(2,1)} %fusion.14), calls=%async_computation | async-start | bytes 7340032 | tf_op jit(solution)/shard_map/all_to_all | solution.py:79
  23.9 47.3 %copy-start = (f32[1,16,14336]{2,1,0:T(8,128)S(1)}, f32[1,16,14336]{2,1,0:T(8,128)}, u32[]{:S(2)}) copy-start(f32[1,16,14336]{2,1,0:T(8,128)} %param.14) | copy-start | bytes 2752516
  74.0 17.1 %all-to-all-start.1 = ((f32[16,1,2]{2,1,0:T(1,128)}), f32[16,1,2]{2,1,0:T(1,128)S(1)}, u32[]{:S(2)}, u32[]{:S(2)}) async-start(f32[16,1,2]{2,1,0:T(1,128)} %broadcast_in_dim.18), calls=%async_computation.1 | async-start | bytes 16384 | tf_op jit(solution)/shard_map/all_to_all | solution.py:16
  81.6 155.4 %all-gather.2.cloned.1.call-start = ((), (), s32[]{:S(2)}) async-start(), calls=%async_computation.2 | async-start | bytes 7798784 | tf_op jit(solution)/shard_map/all_gather | solution.py:117
  86.4 6.5 %copy-start.2 = (f32[6,32]{1,0:T(8,128)S(1)}, f32[6,32]{1,0:T(8,128)}, u32[]{:S(2)}) copy-start(f32[6,32]{1,0:T(8,128)} %param.16) | copy-start | bytes 2308
  86.4 6.5 %copy-start.3 = (f32[32,2]{0,1:T(2,128)S(1)}, f32[32,2]{0,1:T(2,128)}, u32[]{:S(2)}) copy-start(f32[32,2]{0,1:T(2,128)} %param.18) | copy-start | bytes 772
  86.4 6.5 %copy-start.4 = (f32[32]{0:T(128)S(1)}, f32[32]{0:T(128)}, u32[]{:S(2)}) copy-start(f32[32]{0:T(128)} %param.17) | copy-start | bytes 388
  86.5 6.5 %copy-start.5 = (f32[2]{0:T(128)S(1)}, f32[2]{0:T(128)}, u32[]{:S(2)}) copy-start(f32[2]{0:T(128)} %param.19) | copy-start | bytes 28
Sparse Core Ops, SparseCore 0:
  170.7 66.3 all-gather.1
